TPU v7x, 32 devices: a whole 2x2x4 slice. The times are simulated.
32 devices in a mesh: grp: 2 (over y), seq: 4 (over z), ch: 2 (over x), col: 2 (over core).
Axes of the slice: x: 2, y: 2, z: 4, core: 2. Of those that a mesh axis runs over, the one named last changes fastest.
Arguments:
- latent: bfloat16 [8, 4, 16, 512], P('grp', 'seq', 'col', 'ch'), parts along dimension 0, may hold values from -8 to 8, as said below
- mid_gain: float32 [512], P('ch'), may hold values from 0.25 to 1.75
- mid_bias: float32 [512], P('ch'), may hold values from -3 to 3
- mid_weight: bfloat16 [3, 3, 3, 512, 512], P(None, None, None, None, 'ch'), may hold values from -0.0546875 to 0.0546875
- mid_conv_bias: float32 [512], P('ch'), may hold values from -2 to 2
- first_gain: float32 [512], P('ch'), may hold values from 0.25 to 1.75
- first_bias: float32 [512], P('ch'), may hold values from -3 to 3
- first_weight: bfloat16 [3, 3, 3, 512, 512], P(None, None, None, None, 'ch'), may hold values from -0.0546875 to 0.0546875
- first_conv_bias: float32 [512], P('ch'), may hold values from -2 to 2
- second_gain: float32 [512], P('ch'), may hold values from 0.25 to 1.75
- second_bias: float32 [512], P('ch'), may hold values from -3 to 3
- second_weight: bfloat16 [3, 3, 3, 512, 512], P(None, None, None, None, 'ch'), may hold values from -0.0546875 to 0.0546875
- second_conv_bias: float32 [512], P('ch'), may hold values from -2 to 2
Outputs:
- decoded: bfloat16 [16, 4, 16, 512], P(('grp', 'seq'), None, 'col', 'ch'), parts along dimension 0
There are 2 independent parts, one for each index of `grp`. A program takes and returns all parts, laid end to end along the dimension named above; an argument that names none is the same for every part. Nothing has to cross between parts.
Inputs may be any that keep to these rules, and one draw needn't show every extreme that they name: `latent`: each row has its own scale and each row and channel its own offset; values are clipped to the range.
All inputs are finite; a program needn't handle non-finite values.
Results may differ from a plain program's by a relative error of at most 0.0095.
Values may be sent and summed in bfloat16 or wider, within the bound.
A program may use at most 64 MiB of HBM per device.

v0:
```python
import jax
import jax.numpy as jnp
from jax import lax
from jax.sharding import PartitionSpec as P

C = 512
GROUPS = 32


def extended_2(shard, sides, width):
    for axis, dim in sides:
        size, length = (lax.axis_size(axis), shard.shape[dim])
        up = [(i, (i + 1) % size) for i in range(size - 1)]
        down = [(j, i) for i, j in up]
        last = lax.slice_in_dim(shard, length - width, length, axis=dim)
        first = lax.slice_in_dim(shard, 0, width, axis=dim)
        before = lax.ppermute(last, axis, up)
        after = lax.ppermute(first, axis, down)
        shard = jnp.concatenate([before, shard, after], axis=dim)
    return shard


def shifted(value, axis, steps):
    count = lax.axis_size(axis)
    first, last = (max(0, -steps), min(count, count - steps))
    return lax.ppermute(value, axis, [(source, source + steps) for source in range(first, last)])


def group_norm(field, gain, shift_term):
    values = field.astype(jnp.float32)
    group_size = C // GROUPS
    totals = jnp.sum(values, axis=(0, 1, 2)).reshape(-1, group_size).sum(axis=1)
    squares = jnp.sum(values * values, axis=(0, 1, 2)).reshape(-1, group_size).sum(axis=1)
    totals, squares = lax.psum((totals, squares), ("seq", "col"))
    samples = (
        values.shape[0]
        * values.shape[1]
        * values.shape[2]
        * group_size
        * lax.axis_size("seq")
        * lax.axis_size("col")
    )
    group_mean = totals / samples
    spread = squares / samples - group_mean * group_mean
    inverse = 1.0 / jnp.sqrt(spread + 0.01)
    scaled = (values - jnp.repeat(group_mean, group_size)) * jnp.repeat(
        inverse, group_size
    ) * gain + shift_term
    return jax.nn.silu(scaled).astype(jnp.bfloat16)


def spatial_halo(activation):
    return extended_2(activation, (("seq", 1), ("col", 2)), 1)


def causal_pad(extended):
    return jnp.pad(extended, ((2, 0), (0, 0), (0, 0), (0, 0)))


def channel_conv(padded, weight):
    frames_out = padded.shape[0] - 2
    rows_out = padded.shape[1] - 2
    cols_out = padded.shape[2] - 2
    running = jnp.zeros((frames_out, rows_out, cols_out, weight.shape[4]), jnp.float32)
    carried = running
    portion = lax.all_gather(padded, "ch", axis=3, tiled=True)
    for tap_time in range(3):
        for tap_row in range(3):
            for tap_col in range(3):
                window = portion[
                    tap_time : tap_time + frames_out,
                    tap_row : tap_row + rows_out,
                    tap_col : tap_col + cols_out,
                ]
                carried = carried + jnp.einsum(
                    "thwc,co->thwo",
                    window,
                    weight[tap_time, tap_row, tap_col],
                    preferred_element_type=jnp.float32,
                )
    return carried


def to_frames(field):
    return lax.all_to_all(field, "seq", split_axis=0, concat_axis=1, tiled=True)


def frames_conv(activation, weight):
    history = shifted(activation, "seq", 1)
    extended = jnp.concatenate([history, activation], axis=0)
    extended = jnp.pad(extended, ((0, 0), (1, 1), (0, 0), (0, 0)))
    extended = extended_2(extended, (("col", 2),), 1)
    return channel_conv(extended, weight)


def rows_conv(activation, weight):
    return channel_conv(causal_pad(spatial_halo(activation)), weight)


def body(
    latent,
    mid_gain,
    mid_bias,
    mid_weight,
    mid_conv_bias,
    first_gain,
    first_bias,
    first_weight,
    first_conv_bias,
    second_gain,
    second_bias,
    second_weight,
    second_conv_bias,
):
    mid_act = group_norm(latent, mid_gain, mid_bias)
    mixed = rows_conv(mid_act, mid_weight)
    middle = (latent.astype(jnp.float32) + mixed + mid_conv_bias).astype(jnp.bfloat16)
    owned = to_frames(middle)
    doubled = jnp.repeat(owned, 2, axis=0)
    first_act = group_norm(doubled, first_gain, first_bias)
    hidden = (frames_conv(first_act, first_weight) + first_conv_bias).astype(jnp.bfloat16)
    second_act = group_norm(hidden, second_gain, second_bias)
    return (
        doubled.astype(jnp.float32) + frames_conv(second_act, second_weight) + second_conv_bias
    ).astype(jnp.bfloat16)


def solution(mesh):
    in_specs = (
        P("grp", "seq", "col", "ch"),
        P("ch"),
        P("ch"),
        P(None, None, None, None, "ch"),
        P("ch"),
        P("ch"),
        P("ch"),
        P(None, None, None, None, "ch"),
        P("ch"),
        P("ch"),
        P("ch"),
        P(None, None, None, None, "ch"),
        P("ch"),
    )
    out_specs = P(("grp", "seq"), None, "col", "ch")
    return jax.shard_map(body, mesh=mesh, in_specs=in_specs, out_specs=out_specs, check_vma=False)
```

profile of v0, /device:TPU:0, one launch (start us, length us, event | category | flops | bytes accessed | tf_op | source)
XLA Modules:
  0.0 199.4 jit_solution(3506610453255780080)
XLA Ops:
  1.2 18.1 %all-reduce.5 = (f32[16]{0:T(128)S(1)}, f32[16]{0:T(128)S(1)}) all-reduce(f32[16]{0:T(128)S(1)} %reduce_sum.111, f32[16]{0:T(128)S(1)} %reduce_sum.109), channel_id=1, replica_groups=mesh['grp'=2,'seq'=4,'ch'=2,'col'=2] {'seq','col'}, use_global_device_ids=true, to_apply=%region_5.0 | all-reduce | flops 32 | bytes 256 | tf_op jit(solution)/shard_map/psum | solution.py:34
  20.4 1.3 collective-permute-start.1
  21.7 4.5 %collective-permute-start = (bf16[4,1,8,256]{3,2,0,1:T(8,128)(2,1)S(1)}, bf16[4,1,8,256]{3,2,0,1:T(8,128)(2,1)S(1)}, u32[]{:S(2)}, u32[]{:S(2)}) collective-permute-start(bf16[4,1,8,256]{3,2,0,1:T(8,128)(2,1)S(1)} %fusion.251), channel_id=1, source_target_pairs={{0,4},{4,8},{8,12},{1,5},{5,9},{9,13},{2,6},{6,10},{10,14},{3,7},{... | collective-permute-start | bytes 49160 | tf_op jit(solution)/shard_map/ppermute | solution.py:17
  26.3 1.4 collective-permute-done
  27.7 1.3 collective-permute-start.2
  29.0 1.3 collective-permute-start.3
  30.3 1.8 collective-permute-done.3
  32.1 6.6 %all_gather.9 = bf16[6,3,10,512]{3,2,0,1:T(8,128)(2,1)S(1)} all-gather(bf16[6,3,10,256]{3,2,0,1:T(8,128)(2,1)S(1)} %fusion.183), channel_id=1, replica_groups=mesh['grp'=2,'seq'=4,'ch'=2,'col'=2] {'ch'}, dimensions={3}, use_global_device_ids=true | all-gather | bytes 276480 | tf_op jit(solution)/shard_map/all_gather | solution.py:66
  68.9 9.0 %all_to_all.4 = bf16[4,1,8,256]{3,2,1,0:T(8,128)(2,1)S(1)} all-to-all(bf16[4,1,8,256]{3,2,1,0:T(8,128)(2,1)S(1)} %fusion.10), channel_id=1, replica_groups=mesh['grp'=2,'seq'=4,'ch'=2,'col'=2] {'seq'}, dimensions={0} | all-to-all | bytes 32768 | tf_op jit(solution)/shard_map/all_to_all | solution.py:85
  78.3 13.6 %all-reduce.4 = (f32[16]{0:T(128)S(1)}, f32[16]{0:T(128)S(1)}) all-reduce(f32[16]{0:T(128)S(1)} %reduce_sum.115, f32[16]{0:T(128)S(1)} %reduce_sum.113), channel_id=1, replica_groups=mesh['grp'=2,'seq'=4,'ch'=2,'col'=2] {'seq','col'}, use_global_device_ids=true, to_apply=%region_11.12 | all-reduce | flops 32 | bytes 256 | tf_op jit(solution)/shard_map/psum | solution.py:34
  92.3 1.3 collective-permute-start.4
  93.6 1.6 collective-permute-done.4
  95.2 1.3 collective-permute-start.5
  96.5 1.3 collective-permute-start.6
  97.8 1.8 collective-permute-done.6
  99.7 7.6 %all_gather.10 = bf16[4,6,10,512]{3,2,1,0:T(8,128)(2,1)S(1)} all-gather(bf16[4,6,10,256]{3,2,1,0:T(8,128)(2,1)S(1)} %pad_maximum_fusion), channel_id=1, replica_groups=mesh['grp'=2,'seq'=4,'ch'=2,'col'=2] {'ch'}, dimensions={3}, use_global_device_ids=true | all-gather | bytes 368640 | tf_op jit(solution)/shard_map/all_gather | solution.py:66
  108.4 1.1 convolution_add_fusion.51
  109.6 1.1 convolution_add_fusion.50
  111.8 1.1 convolution_add_fusion.48
  113.0 1.1 convolution_add_fusion.47
  115.2 1.1 convolution_add_fusion.45
  116.3 1.1 convolution_add_fusion.44
  118.6 1.1 convolution_add_fusion.42
  119.7 1.1 convolution_add_fusion.41
  122.0 1.1 convolution_add_fusion.39
  124.2 1.1 convolution_add_fusion.37
  125.3 1.1 convolution_add_fusion.36
  129.9 1.1 convolution_add_fusion.32
  133.2 1.1 convolution_add_fusion.29
  135.5 1.1 convolution_add_fusion.27
  136.6 1.1 fusion.254
  138.2 14.8 %all-reduce.3 = (f32[16]{0:T(128)S(1)}, f32[16]{0:T(128)S(1)}) all-reduce(f32[16]{0:T(128)S(1)} %reduce_sum.119, f32[16]{0:T(128)S(1)} %reduce_sum.117), channel_id=1, replica_groups=mesh['grp'=2,'seq'=4,'ch'=2,'col'=2] {'seq','col'}, use_global_device_ids=true, to_apply=%region_17.18 | all-reduce | flops 32 | bytes 256 | tf_op jit(solution)/shard_map/psum | solution.py:34
  153.3 1.3 collective-permute-start.7
  154.6 1.6 collective-permute-done.7
  156.3 1.3 collective-permute-start.8
  157.6 1.3 collective-permute-start.9
  158.9 1.8 collective-permute-done.9
  160.8 7.6 %all_gather.11 = bf16[4,6,10,512]{3,2,1,0:T(8,128)(2,1)S(1)} all-gather(bf16[4,6,10,256]{3,2,1,0:T(8,128)(2,1)S(1)} %pad_maximum_fusion.1), channel_id=1, replica_groups=mesh['grp'=2,'seq'=4,'ch'=2,'col'=2] {'ch'}, dimensions={3}, use_global_device_ids=true | all-gather | bytes 368640 | tf_op jit(solution)/shard_map/all_gather | solution.py:66
  169.5 1.1 convolution_add_fusion.25
  172.9 1.1 convolution_add_fusion.22
  174.0 1.1 convolution_add_fusion.21
  176.3 1.1 convolution_add_fusion.19
  179.6 1.1 convolution_add_fusion.16
  185.3 1.1 convolution_add_fusion.11
  187.5 1.1 convolution_add_fusion.9
  190.9 1.1 convolution_add_fusion.6
  196.5 1.1 convolution_add_fusion.1
  197.7 1.7 fusion.5
  (119 shorter events, 66.7 us)
Async XLA Ops:
  0.0 67.7 %copy-start = (bf16[4,1,8,256]{3,2,1,0:T(8,128)(2,1)S(1)}, bf16[4,1,8,256]{3,2,1,0:T(8,128)(2,1)}, u32[]{:S(2)}) copy-start(bf16[4,1,8,256]{3,2,1,0:T(8,128)(2,1)} %param.13) | copy-start | bytes 49156
  0.0 67.7 %copy-start.5 = (f32[256]{0:T(256)S(1)}, f32[256]{0:T(256)}, u32[]{:S(2)}) copy-start(f32[256]{0:T(256)} %param.17) | copy-start | bytes 3076
  0.0 92.2 %copy-start.1 = (f32[256]{0:T(256)S(1)}, f32[256]{0:T(256)}, u32[]{:S(2)}) copy-start(f32[256]{0:T(256)} %param.19) | copy-start | bytes 3076
  0.0 92.2 %copy-start.2 = (f32[256]{0:T(256)S(1)}, f32[256]{0:T(256)}, u32[]{:S(2)}) copy-start(f32[256]{0:T(256)} %param.18) | copy-start | bytes 3076
  20.4 5.9 %collective-permute-start.1 = (bf16[4,1,8,256]{3,2,0,1:T(8,128)(2,1)S(1)}, bf16[4,1,8,256]{3,2,0,1:T(8,128)(2,1)S(1)}, u32[]{:S(2)}, u32[]{:S(2)}) collective-permute-start(bf16[4,1,8,256]{3,2,0,1:T(8,128)(2,1)S(1)} %fusion.251), channel_id=1, source_target_pairs={{4,0},{8,4},{12,8},{5,1},{9,5},{13,9},{6,2},{10,6},{14,10},{7,3},{... | collective-permute-start | bytes 49160 | tf_op jit(solution)/shard_map/ppermute | solution.py:18
  21.7 6.0 %collective-permute-start = (bf16[4,1,8,256]{3,2,0,1:T(8,128)(2,1)S(1)}, bf16[4,1,8,256]{3,2,0,1:T(8,128)(2,1)S(1)}, u32[]{:S(2)}, u32[]{:S(2)}) collective-permute-start(bf16[4,1,8,256]{3,2,0,1:T(8,128)(2,1)S(1)} %fusion.251), channel_id=1, source_target_pairs={{0,4},{4,8},{8,12},{1,5},{5,9},{9,13},{2,6},{6,10},{10,14},{3,7},{... | collective-permute-start | bytes 49160 | tf_op jit(solution)/shard_map/ppermute | solution.py:17
  27.7 2.6 %collective-permute-start.2 = (bf16[4,3,1,256]{3,2,0,1:T(2,128)(2,1)S(1)}, bf16[4,3,1,256]{3,2,0,1:T(2,128)(2,1)S(1)}, u32[]{:S(2)}, u32[]{:S(2)}) collective-permute-start(bf16[4,3,1,256]{3,2,0,1:T(2,128)(2,1)S(1)} %get-tuple-element.19), channel_id=1, source_target_pairs={{0,1},{2,3},{4,5},{6,7},{8,9},{10,11},{12,13},{14,15},{16,17},{18,... | collective-permute-start | bytes 18440 | tf_op jit(solution)/shard_map/ppermute | solution.py:17
  29.0 3.1 %collective-permute-start.3 = (bf16[4,3,1,256]{3,2,0,1:T(2,128)(2,1)S(1)}, bf16[4,3,1,256]{3,2,0,1:T(2,128)(2,1)S(1)}, u32[]{:S(2)}, u32[]{:S(2)}) collective-permute-start(bf16[4,3,1,256]{3,2,0,1:T(2,128)(2,1)S(1)} %get-tuple-element.20), channel_id=1, source_target_pairs={{1,0},{3,2},{5,4},{7,6},{9,8},{11,10},{13,12},{15,14},{17,16},{19,... | collective-permute-start | bytes 18440 | tf_op jit(solution)/shard_map/ppermute | solution.py:18
  66.6 70.1 %copy-start.6 = (f32[256]{0:T(256)S(1)}, f32[256]{0:T(256)}, u32[]{:S(2)}) copy-start(f32[256]{0:T(256)} %param.21) | copy-start | bytes 3076
  68.8 84.4 %copy-start.3 = (f32[256]{0:T(256)S(1)}, f32[256]{0:T(256)}, u32[]{:S(2)}) copy-start(f32[256]{0:T(256)} %param.23) | copy-start | bytes 3076
  68.8 84.4 %copy-start.4 = (f32[256]{0:T(256)S(1)}, f32[256]{0:T(256)}, u32[]{:S(2)}) copy-start(f32[256]{0:T(256)} %param.22) | copy-start | bytes 3076
  92.3 2.9 %collective-permute-start.4 = (bf16[2,4,8,256]{3,2,1,0:T(8,128)(2,1)S(1)}, bf16[2,4,8,256]{3,2,1,0:T(8,128)(2,1)S(1)}, u32[]{:S(2)}, u32[]{:S(2)}) collective-permute-start(bf16[2,4,8,256]{3,2,1,0:T(8,128)(2,1)S(1)} %multiply_convert_fusion.1), channel_id=1, source_target_pairs={{0,4},{4,8},{8,12},{1,5},{5,9},{9,13},{2,6},{6,10},{10,14},{3,7},{... | collective-permute-start | bytes 98312 | tf_op jit(solution)/shard_map/ppermute | solution.py:26
  95.2 2.6 %collective-permute-start.5 = (bf16[4,6,1,256]{3,2,1,0:T(2,128)(2,1)S(1)}, bf16[4,6,1,256]{3,2,1,0:T(2,128)(2,1)S(1)}, u32[]{:S(2)}, u32[]{:S(2)}) collective-permute-start(bf16[4,6,1,256]{3,2,1,0:T(2,128)(2,1)S(1)} %get-tuple-element.17), channel_id=1, source_target_pairs={{0,1},{2,3},{4,5},{6,7},{8,9},{10,11},{12,13},{14,15},{16,17},{18,... | collective-permute-start | bytes 36872 | tf_op jit(solution)/shard_map/ppermute | solution.py:17
  96.5 3.1 %collective-permute-start.6 = (bf16[4,6,1,256]{3,2,1,0:T(2,128)(2,1)S(1)}, bf16[4,6,1,256]{3,2,1,0:T(2,128)(2,1)S(1)}, u32[]{:S(2)}, u32[]{:S(2)}) collective-permute-start(bf16[4,6,1,256]{3,2,1,0:T(2,128)(2,1)S(1)} %get-tuple-element.18), channel_id=1, source_target_pairs={{1,0},{3,2},{5,4},{7,6},{9,8},{11,10},{13,12},{15,14},{17,16},{19,... | collective-permute-start | bytes 36872 | tf_op jit(solution)/shard_map/ppermute | solution.py:18
  135.5 62.2 %copy-start.7 = (f32[256]{0:T(256)S(1)}, f32[256]{0:T(256)}, u32[]{:S(2)}) copy-start(f32[256]{0:T(256)} %param.25) | copy-start | bytes 3076
  153.3 2.9 %collective-permute-start.7 = (bf16[2,4,8,256]{3,2,1,0:T(8,128)(2,1)S(1)}, bf16[2,4,8,256]{3,2,1,0:T(8,128)(2,1)S(1)}, u32[]{:S(2)}, u32[]{:S(2)}) collective-permute-start(bf16[2,4,8,256]{3,2,1,0:T(8,128)(2,1)S(1)} %multiply_convert_fusion), channel_id=1, source_target_pairs={{0,4},{4,8},{8,12},{1,5},{5,9},{9,13},{2,6},{6,10},{10,14},{3,7},{... | collective-permute-start | bytes 98312 | tf_op jit(solution)/shard_map/ppermute | solution.py:26
  156.3 2.6 %collective-permute-start.8 = (bf16[4,6,1,256]{3,2,1,0:T(2,128)(2,1)S(1)}, bf16[4,6,1,256]{3,2,1,0:T(2,128)(2,1)S(1)}, u32[]{:S(2)}, u32[]{:S(2)}) collective-permute-start(bf16[4,6,1,256]{3,2,1,0:T(2,128)(2,1)S(1)} %get-tuple-element.15), channel_id=1, source_target_pairs={{0,1},{2,3},{4,5},{6,7},{8,9},{10,11},{12,13},{14,15},{16,17},{18,... | collective-permute-start | bytes 36872 | tf_op jit(solution)/shard_map/ppermute | solution.py:17
  157.6 3.1 %collective-permute-start.9 = (bf16[4,6,1,256]{3,2,1,0:T(2,128)(2,1)S(1)}, bf16[4,6,1,256]{3,2,1,0:T(2,128)(2,1)S(1)}, u32[]{:S(2)}, u32[]{:S(2)}) collective-permute-start(bf16[4,6,1,256]{3,2,1,0:T(2,128)(2,1)S(1)} %get-tuple-element.16), channel_id=1, source_target_pairs={{1,0},{3,2},{5,4},{7,6},{9,8},{11,10},{13,12},{15,14},{17,16},{19,... | collective-permute-start | bytes 36872 | tf_op jit(solution)/shard_map/ppermute | solution.py:18
where the time goes:
time: 202 us; the launch traced here: 199 us
  matrix products  91.3 us (45%)
  blocking collectives  77.3 us (38%)
  starting transfers between devices  16.2 us (8%)
  waiting for transfers between devices  9.9 us (5%)
  other arithmetic  2.75 us (1%)
    dot_general x81, matrix products, channel_conv(): jnp.einsum('thwc,co->thwo', window, weight[tap_time, tap_row, tap_col], p...  91.3 us
    psum x3, blocking collectives, group_norm(): totals, squares = lax.psum((totals, squares), ('seq', 'col'))  46.5 us
    all_gather x3, blocking collectives, channel_conv(): portion = lax.all_gather(padded, 'ch', axis=3, tiled=True)  21.9 us
    all_to_all x1, blocking collectives, to_frames(): return lax.all_to_all(field, 'seq', split_axis=0, concat_axis=1, tiled=True)  8.98 us
    ppermute x4, starting transfers between devices, extended_2(): before = lax.ppermute(last, axis, up)  8.42 us
    ppermute x4, waiting for transfers between devices, extended_2(): after = lax.ppermute(first, axis, down)  5.32 us
    ppermute x4, starting transfers between devices, extended_2(): after = lax.ppermute(first, axis, down)  5.17 us
  transfers between devices with their start and end apart: 10, of which 6 were waited for; matrix products, arithmetic and copies ran while one was open for 0% of the time, Pallas kernels for 0%

commit v1 on v0

v1 whole, which is shorter than its diff:
```python
import functools

import jax
import jax.numpy as jnp
from jax import lax
from jax.experimental import pallas as pl
from jax.experimental.pallas import tpu as pltpu
from jax.sharding import PartitionSpec as P

GROUPS = 32
MESH = pl.DeviceIdType.MESH
F32 = jnp.float32
BF16 = jnp.bfloat16


def each(count, visit):
    if count <= 16:
        for i in range(count):
            visit(i)
    else:
        lax.fori_loop(0, count, lambda i, carry: (visit(i), carry)[1], 0)


def kernel(
    sizes,
    latent,
    mid_gain, mid_bias, mid_conv_bias,
    first_gain, first_bias, first_conv_bias,
    second_gain, second_bias, second_conv_bias,
    mid_weight, first_weight, second_weight,
    out,
    w0, w1, w2, w_sem,
    act0, act1, act2,
    params, stat, packed, group_ref,
    lat, lat_edge_src, lat_edge,
    mid_src, mid_edge_src, mid, mid_edge,
    hid_src, hid_edge_src, hid, hid_edge,
    par_send, par_recv, stat_send, stat_recv,
    lat_send, lat_recv, late_send, late_recv,
    mid_send, mid_recv, mide_send, mide_recv,
    hid_send, hid_recv, hide_send, hide_recv,
):
    ns, nh, nk, frames, width, chans, group_size = sizes
    rows = ns
    n, pairs, spread_over = ns * nh * nk, ns * nh, ns * nk
    s, h, k = lax.axis_index("seq"), lax.axis_index("ch"), lax.axis_index("col")
    other = 1 - k
    me = h * spread_over + s * nk + k

    def coords(flat):
        return {"ch": flat // spread_over, "seq": (flat % spread_over) // nk, "col": flat % nk}

    barrier = pltpu.get_barrier_semaphore()

    def greet(i):
        pl.semaphore_signal(barrier, inc=1, device_id=coords((me + i + 1) % n), device_id_type=MESH)

    each(n - 1, greet)

    loads = []
    for c, (source, target) in enumerate(((mid_weight, w0), (first_weight, w1), (second_weight, w2))):
        for dt in range(3):
            load = pltpu.make_async_copy(source.at[dt], target.at[dt], w_sem.at[c, dt])
            load.start()
            loads.append(load)

    def send(src, dst, send_sem, recv_sem, where):
        pltpu.make_async_remote_copy(
            src_ref=src, dst_ref=dst, send_sem=send_sem, recv_sem=recv_sem,
            device_id=where, device_id_type=MESH,
        ).start()

    def take(ref, sem):
        pltpu.make_async_copy(ref, ref, sem).wait()

    def own_stats(step, values):
        flat = values.reshape(-1, chans)
        stat[step, me, 0:1, :] = jnp.sum(flat, axis=0, keepdims=True)
        stat[step, me, 1:2, :] = jnp.sum(flat * flat, axis=0, keepdims=True)

    def send_stats(step):
        def visit(i):
            send(stat.at[step, me], stat.at[step, me], stat_send.at[step], stat_recv.at[step],
                 coords((me + i + 1) % n))
        each(n - 1, visit)

    def edge_of(values):
        return jnp.where(k == 0, values[:, width - 1:width, :], values[:, 0:1, :])

    tile = latent[...].reshape(frames, width, chans)
    values = tile.astype(F32)
    lat[1, h] = tile
    lat_edge_src[...] = edge_of(values)
    own_stats(0, values)
    for row, ref in enumerate((mid_gain, mid_bias, first_gain, first_bias, second_gain, second_bias)):
        params[h, row:row + 1, :] = ref[...].reshape(1, chans)

    pl.semaphore_wait(barrier, n - 1)

    send_stats(0)
    for d in range(1, nh):
        there = {"seq": s, "ch": (h + d) % nh, "col": k}
        send(params.at[h], params.at[h], par_send, par_recv, there)

    def near(steps, ring):
        if steps == 0:
            ring()
        else:
            pl.when((s + steps >= 0) & (s + steps < ns))(ring)

    for slot in range(3):
        def ring(slot=slot):
            steps = 1 - slot
            for d in range(0 if steps else 1, nh):
                there = {"seq": s + steps, "ch": (h + d) % nh, "col": k}
                send(lat.at[1, h], lat.at[slot, h], lat_send.at[slot], lat_recv.at[slot], there)
            for d in range(nh):
                there = {"seq": s + steps, "ch": (h + d) % nh, "col": other}
                send(lat_edge_src, lat_edge.at[slot, h], late_send.at[slot], late_recv.at[slot], there)
        near(1 - slot, ring)

    act0[...] = jnp.zeros_like(act0)
    act1[...] = jnp.zeros_like(act1)
    act2[...] = jnp.zeros_like(act2)
    packed[...] = jnp.zeros_like(packed)
    mid_src[0] = jnp.zeros((width, chans), BF16)
    mid_edge_src[0] = jnp.zeros((1, chans), F32)
    here = lax.broadcasted_iota(jnp.int32, (chans, chans), 0) // group_size
    there = lax.broadcasted_iota(jnp.int32, (chans, chans), 1) // group_size
    group_ref[...] = jnp.where(here == there, 1.0, 0.0).astype(BF16)

    def norm_terms(step, samples):
        take(stat.at[step, pl.ds(0, n - 1)], stat_recv.at[step])
        for j in range(nh):
            packed[2 * j:2 * j + 2, :] = jnp.sum(stat[step, j * spread_over:(j + 1) * spread_over], axis=0)
        exact = packed[...]
        high = exact.astype(BF16)
        rest = exact - high.astype(F32)
        middle = rest.astype(BF16)
        low = (rest - middle.astype(F32)).astype(BF16)
        group = group_ref[...]
        total = sum(jnp.dot(part, group, preferred_element_type=F32) for part in (low, middle, high))
        terms = []
        for j in range(nh):
            mean = total[2 * j:2 * j + 1] / samples
            square = total[2 * j + 1:2 * j + 2] / samples
            inverse = 1.0 / jnp.sqrt(square - mean * mean + 0.01)
            gain = params[j, 2 * step:2 * step + 1, :]
            shift = params[j, 2 * step + 1:2 * step + 2, :]
            terms.append((mean, inverse * gain, shift))
        return terms

    def activate(values, term):
        mean, scale, shift = term
        scaled = (values.astype(F32) - mean) * scale + shift
        return scaled / (1.0 + jnp.exp(-scaled))

    def place(target, index, j, values, edge, term):
        centre = activate(values, term)
        side = activate(edge, term)
        left = jnp.where(k == 1, side, 0.0)
        right = jnp.where(k == 0, side, 0.0)
        column = lax.broadcasted_iota(jnp.int32, centre.shape, 1)
        lanes = slice(j * chans, (j + 1) * chans)
        before = jnp.where(column == 0, left, pltpu.roll(centre, 1, 1))
        after = jnp.where(column == width - 1, right, pltpu.roll(centre, width - 1, 1))
        for dj, moved in enumerate((before, centre, after)):
            target[(dj,) + index + (slice(None), lanes)] = moved

    def taps(window, weight, dt):
        total = None
        for di in range(3):
            for dj in range(3):
                lhs = window(di, dj)
                lhs = lhs.reshape(-1, lhs.shape[-1]).astype(BF16)
                part = jnp.dot(lhs, weight[dt, di, dj], preferred_element_type=F32)
                total = part if total is None else total + part
        return total

    take(params.at[pl.ds(0, nh - 1)], par_recv)
    terms = norm_terms(0, frames * width * group_size * spread_over)
    for slot in range(3):
        def fill(slot=slot):
            if slot == 1:
                take(lat.at[slot, pl.ds(0, nh - 1)], lat_recv.at[slot])
            else:
                take(lat.at[slot], lat_recv.at[slot])
            take(lat_edge.at[slot], late_recv.at[slot])
            for j in range(nh):
                place(act0, (slice(2, 2 + frames), slot), j, lat[slot, j], lat_edge[slot, j], terms[j])
        near(slot - 1, fill)
    mixed = None
    for dt in range(3):
        loads[dt].wait()
        part = taps(lambda di, dj: act0[dj, dt:dt + frames, di], w0, dt)
        mixed = part if mixed is None else mixed + part
    summed = values.reshape(-1, chans) + mixed + mid_conv_bias[...].reshape(1, chans)
    tile = summed.astype(BF16).reshape(frames, width, chans)
    values = tile.astype(F32)
    mid_src[1:1 + frames] = tile
    mid_edge_src[1:1 + frames] = edge_of(values)
    own_stats(1, values)
    slot_here = h * ns + s

    def send_mid(i):
        q = (slot_here + i + 1) % pairs
        send(mid_src.at[pl.ds(q % ns, 2)], mid.at[slot_here], mid_send, mid_recv,
             {"seq": q % ns, "ch": q // ns, "col": k})

    def send_mid_edge(i):
        q = (slot_here + i) % pairs
        send(mid_edge_src.at[pl.ds(q % ns, 2)], mid_edge.at[slot_here], mide_send, mide_recv,
             {"seq": q % ns, "ch": q // ns, "col": other})

    each(pairs - 1, send_mid)
    each(pairs, send_mid_edge)
    send_stats(1)
    mid[slot_here] = mid_src[pl.ds(s, 2)]

    terms = norm_terms(1, frames * width * group_size * spread_over)
    take(mid.at[pl.ds(0, pairs - 1)], mid_recv)
    take(mid_edge, mide_recv)

    def fill_frame(f):
        for j in range(nh):
            place(act1, (f, slice(1, 1 + rows)), j, mid[j * ns:(j + 1) * ns, f],
                  mid_edge[j * ns:(j + 1) * ns, f], terms[j])

    pl.when(s > 0)(lambda: fill_frame(0))
    fill_frame(1)
    for dt in range(3):
        loads[3 + dt].wait()
    half = rows * width
    oldest = taps(lambda di, dj: act1[dj, 0, di:di + rows], w1, 0)
    both = taps(lambda di, dj: act1[dj, :, di:di + rows], w1, 1)
    newest = taps(lambda di, dj: act1[dj, 1, di:di + rows], w1, 2)
    shared = oldest + newest + first_conv_bias[...].reshape(1, chans)
    summed = jnp.concatenate([shared + both[:half], shared + both[half:]], axis=0)
    tile = summed.astype(BF16).reshape(2 * rows, width, chans)
    values = tile.astype(F32)
    hid_src[...] = tile
    hid_edge_src[...] = edge_of(values)
    own_stats(2, values)
    for slot in (1, 0):
        def ring(slot=slot):
            steps = 1 - slot
            for d in range(0 if steps else 1, nh):
                there = {"seq": s + steps, "ch": (h + d) % nh, "col": k}
                send(hid_src, hid.at[slot, h], hid_send.at[slot], hid_recv.at[slot], there)
            for d in range(nh):
                there = {"seq": s + steps, "ch": (h + d) % nh, "col": other}
                send(hid_edge_src, hid_edge.at[slot, h], hide_send.at[slot], hide_recv.at[slot], there)
        near(1 - slot, ring)
    send_stats(2)
    hid[1, h] = tile

    terms = norm_terms(2, 2 * rows * width * group_size * spread_over)
    for slot in (1, 0):
        def fill(slot=slot):
            if slot == 1:
                take(hid.at[slot, pl.ds(0, nh - 1)], hid_recv.at[slot])
            else:
                take(hid.at[slot], hid_recv.at[slot])
            take(hid_edge.at[slot], hide_recv.at[slot])
            for j in range(nh):
                for f in range(2):
                    part = slice(f * rows, (f + 1) * rows)
                    place(act2, (2 * slot + f, slice(1, 1 + rows)), j, hid[slot, j, part],
                          hid_edge[slot, j, part], terms[j])
        near(slot - 1, fill)
    mixed = None
    for dt in range(3):
        loads[6 + dt].wait()
        part = taps(lambda di, dj: act2[dj, dt:dt + 2, di:di + rows], w2, dt)
        mixed = part if mixed is None else mixed + part
    mixed = mixed + second_conv_bias[...].reshape(1, chans)
    kept = mid[pl.ds(h * ns, ns), 1].astype(F32).reshape(half, chans)
    for f in range(2):
        whole = kept + mixed[f * half:(f + 1) * half]
        out[f] = whole.astype(BF16).reshape(rows, width, chans)

    for step in range(3):
        take(stat.at[step, pl.ds(0, n - 1)], stat_send.at[step])
    take(params.at[pl.ds(0, nh - 1)], par_send)
    take(mid.at[pl.ds(0, pairs - 1)], mid_send)
    take(mid_edge, mide_send)
    for slot in range(3):
        def left(slot=slot):
            if slot == 1:
                take(lat.at[slot, pl.ds(0, nh - 1)], lat_send.at[slot])
            else:
                take(lat.at[slot], lat_send.at[slot])
            take(lat_edge.at[slot], late_send.at[slot])
        near(1 - slot, left)
    for slot in (1, 0):
        def left(slot=slot):
            if slot == 1:
                take(hid.at[slot, pl.ds(0, nh - 1)], hid_send.at[slot])
            else:
                take(hid.at[slot], hid_send.at[slot])
            take(hid_edge.at[slot], hide_send.at[slot])
        near(1 - slot, left)


def solution(mesh):
    ns, nh, nk = mesh.shape["seq"], mesh.shape["ch"], mesh.shape["col"]

    def body(
        latent,
        mid_gain, mid_bias, mid_weight, mid_conv_bias,
        first_gain, first_bias, first_weight, first_conv_bias,
        second_gain, second_bias, second_weight, second_conv_bias,
    ):
        frames, own_rows, width, chans = latent.shape
        assert nk == 2 and own_rows == 1 and frames == ns
        rows = ns
        full = chans * nh
        sizes = (ns, nh, nk, frames, width, chans, full // GROUPS)
        n, pairs = ns * nh * nk, ns * nh
        vmem = pl.BlockSpec(memory_space=pltpu.VMEM)
        hbm = pl.BlockSpec(memory_space=pl.ANY)
        dma = pltpu.SemaphoreType.DMA
        taps = mid_weight.shape
        return pl.pallas_call(
            functools.partial(kernel, sizes),
            out_shape=jax.ShapeDtypeStruct((2, rows, width, chans), BF16),
            in_specs=[vmem] * 10 + [hbm] * 3,
            out_specs=vmem,
            scratch_shapes=[
                pltpu.VMEM(taps, BF16), pltpu.VMEM(taps, BF16), pltpu.VMEM(taps, BF16), dma((3, 3)),
                pltpu.VMEM((3, frames + 2, 3, width, full), F32),
                pltpu.VMEM((3, 2, rows + 2, width, full), F32),
                pltpu.VMEM((3, 4, rows + 2, width, full), F32),
                pltpu.VMEM((nh, 8, chans), F32),
                pltpu.VMEM((3, n, 2, chans), F32),
                pltpu.VMEM((max(8, 2 * nh), chans), F32),
                pltpu.VMEM((chans, chans), BF16),
                pltpu.VMEM((3, nh, frames, width, chans), BF16),
                pltpu.VMEM((frames, 1, chans), F32),
                pltpu.VMEM((3, nh, frames, 1, chans), F32),
                pltpu.VMEM((frames + 1, width, chans), BF16),
                pltpu.VMEM((frames + 1, 1, chans), F32),
                pltpu.VMEM((pairs, 2, width, chans), BF16),
                pltpu.VMEM((pairs, 2, 1, chans), F32),
                pltpu.VMEM((2 * rows, width, chans), BF16),
                pltpu.VMEM((2 * rows, 1, chans), F32),
                pltpu.VMEM((2, nh, 2 * rows, width, chans), BF16),
                pltpu.VMEM((2, nh, 2 * rows, 1, chans), F32),
                dma, dma, dma((3,)), dma((3,)),
                dma((3,)), dma((3,)), dma((3,)), dma((3,)),
                dma, dma, dma, dma,
                dma((2,)), dma((2,)), dma((2,)), dma((2,)),
            ],
            compiler_params=pltpu.CompilerParams(
                collective_id=0, has_side_effects=True, vmem_limit_bytes=60 * 1024 * 1024
            ),
        )(
            latent,
            mid_gain, mid_bias, mid_conv_bias,
            first_gain, first_bias, first_conv_bias,
            second_gain, second_bias, second_conv_bias,
            mid_weight, first_weight, second_weight,
        )

    vector, weight = P("ch"), P(None, None, None, None, "ch")
    in_specs = (P("grp", "seq", "col", "ch"),) + (vector, vector, weight, vector) * 3
    out_specs = P(("grp", "seq"), None, "col", "ch")
    return jax.shard_map(body, mesh=mesh, in_specs=in_specs, out_specs=out_specs, check_vma=False)
```

time: 202 us -> 29 us (0.14); the launches traced: 199 us -> 28.8 us
  matrix products: 91.3 us -> 0 us
  blocking collectives: 77.3 us -> 0 us
  Pallas kernels: 0 us -> 27.4 us
  starting transfers between devices: 16.2 us -> 0 us
  waiting for transfers between devices: 9.9 us -> 0 us
  other arithmetic: 2.75 us -> 0 us
    dot_general x81 -> x0, matrix products: 91.3 us -> none  [channel_conv(): jnp.einsum('thwc,co->thwo', window, weight[tap_time, tap_row, tap_col], p...]
    psum x3 -> x0, blocking collectives: 46.5 us -> none  [group_norm(): totals, squares = lax.psum((totals, squares), ('seq', 'col'))]
    pallas_call x0 -> x1, Pallas kernels: none -> 27.4 us  [body(): pl.pallas_call(functools.partial(kernel, sizes), out_shape=jax.ShapeDtype...]
    all_gather x3 -> x0, blocking collectives: 21.9 us -> none  [channel_conv(): portion = lax.all_gather(padded, 'ch', axis=3, tiled=True)]
    ppermute x10 -> x0, starting transfers between devices: 16.2 us -> none  [the longest x4 8.42 us: extended_2(): before = lax.ppermute(last, axis, up)]
    ppermute x10 -> x0, waiting for transfers between devices: 9.9 us -> none  [the longest x4 5.32 us: extended_2(): after = lax.ppermute(first, axis, down)]
    all_to_all x1 -> x0, blocking collectives: 8.98 us -> none  [to_frames(): return lax.all_to_all(field, 'seq', split_axis=0, concat_axis=1, tiled=True)]
  transfers between devices with their start and end apart: 10 -> 0, of which waited for: 6 -> 0; matrix products, arithmetic and copies ran while one was open for 0% -> 0% of each run, Pallas kernels for 0% -> 0%
where the time goes in v1:
time: 29 us; the launch traced here: 28.8 us
  Pallas kernels  27.4 us (94%)
  local copies, waits for them, and re-layouts  1.38 us (5%)
    pallas_call x1, Pallas kernels, body(): pl.pallas_call(functools.partial(kernel, sizes), out_shape=jax.ShapeDtype...  27.4 us
    unnamed x1, local copies, waits for them, and re-layouts  1.38 us

profile of v1, /device:TPU:0, one launch (start us, length us, event | category | flops | bytes accessed | tf_op | source)
XLA Modules:
  0.0 28.8 jit_solution(3186948678422430881)
XLA Ops:
  0.0 27.4 %shard_map.127 = bf16[2,4,8,256]{3,2,1,0:T(8,128)(2,1)} custom-call(bf16[4,1,8,256]{3,2,1,0:T(8,128)(2,1)} %latent.1, f32[256]{0:T(256)} %mid_gain.1, f32[256]{0:T(256)} %mid_bias.1, f32[256]{0:T(256)} %mid_conv_bias.1, f32[256]{0:T(256)} %first_gain.1, f32[256]{0:T(256)} %first_bias.1, f32[256]{0:T(256)} %first_conv_bias.1, f32[256]{0:T(256)} %second_gain.1, ...), custom_call_target="tpu_custom_call" | custom-call | tf_op jit(solution)/shard_map/pallas_call | solution.py:324
  27.4 1.4 %copy.15 = bf16[2,4,8,256]{3,2,1,0:T(8,128)(2,1)} copy(bf16[2,4,8,256]{3,2,1,0:T(8,128)(2,1)} %shard_map.127) | data formatting | bytes 65536

commit v2 on v1

--- a/solution.py
+++ b/solution.py
@@ -14,7 +14,7 @@
 
 
 def each(count, visit):
-    if count <= 16:
+    if count <= 4:
         for i in range(count):
             visit(i)
     else:
@@ -23,12 +23,14 @@
 
 def kernel(
     sizes,
-    latent,
-    mid_gain, mid_bias, mid_conv_bias,
-    first_gain, first_bias, first_conv_bias,
-    second_gain, second_bias, second_conv_bias,
-    mid_weight, first_weight, second_weight,
-    out,
+    *refs,
+):
+    smalls, (mid_weight, first_weight, second_weight), (out,) = refs[:10], refs[10:13], refs[13:14]
+    latent, *vectors = refs[14:24]
+    (mid_gain, mid_bias, mid_conv_bias, first_gain, first_bias, first_conv_bias,
+     second_gain, second_bias, second_conv_bias) = vectors
+    (
+    small_sem,
     w0, w1, w2, w_sem,
     act0, act1, act2,
     params, stat, packed, group_ref,
@@ -39,7 +41,7 @@
     lat_send, lat_recv, late_send, late_recv,
     mid_send, mid_recv, mide_send, mide_recv,
     hid_send, hid_recv, hide_send, hide_recv,
-):
+    ) = refs[24:]
     ns, nh, nk, frames, width, chans, group_size = sizes
     rows = ns
     n, pairs, spread_over = ns * nh * nk, ns * nh, ns * nk
@@ -47,15 +49,39 @@
     other = 1 - k
     me = h * spread_over + s * nk + k
 
-    def coords(flat):
-        return {"ch": flat // spread_over, "seq": (flat % spread_over) // nk, "col": flat % nk}
+    def wrap(index, count):
+        return jnp.where(index >= count, index - count, index)
+
+    def visit_all(visit):
+        down = s < ns // 2
+        def one(i):
+            row = jnp.where(down, ns - 1 - i, i)
+            for dh in reversed(range(nh)):
+                for dk in range(nk):
+                    visit(row, dh, dk)
+        each(ns, one)
+
+    def others(row, dh, dk, act):
+        if dh == 0 and dk == 0:
+            pl.when(row != s)(act)
+        else:
+            act()
+
+    def place_of(row, dh, dk):
+        return {"seq": row, "ch": wrap(h + dh, nh), "col": k if dk == 0 else other}
 
     barrier = pltpu.get_barrier_semaphore()
 
-    def greet(i):
-        pl.semaphore_signal(barrier, inc=1, device_id=coords((me + i + 1) % n), device_id_type=MESH)
-
-    each(n - 1, greet)
+    def greet(row, dh, dk):
+        others(row, dh, dk, lambda: pl.semaphore_signal(
+            barrier, inc=1, device_id=place_of(row, dh, dk), device_id_type=MESH))
+
+    visit_all(greet)
+    small_loads = []
+    for i, (source, target) in enumerate(zip(smalls, [latent] + vectors)):
+        load = pltpu.make_async_copy(source, target, small_sem.at[i])
+        load.start()
+        small_loads.append(load)
 
     loads = []
     for c, (source, target) in enumerate(((mid_weight, w0), (first_weight, w1), (second_weight, w2))):
@@ -78,14 +104,16 @@
         stat[step, me, 0:1, :] = jnp.sum(flat, axis=0, keepdims=True)
         stat[step, me, 1:2, :] = jnp.sum(flat * flat, axis=0, keepdims=True)
 
-    def send_stats(step):
-        def visit(i):
-            send(stat.at[step, me], stat.at[step, me], stat_send.at[step], stat_recv.at[step],
-                 coords((me + i + 1) % n))
-        each(n - 1, visit)
+    def send_stats(step, row, dh, dk):
+        others(row, dh, dk, lambda: send(
+            stat.at[step, me], stat.at[step, me], stat_send.at[step], stat_recv.at[step],
+            place_of(row, dh, dk)))
 
     def edge_of(values):
         return jnp.where(k == 0, values[:, width - 1:width, :], values[:, 0:1, :])
+
+    for load in small_loads:
+        load.wait()
 
     tile = latent[...].reshape(frames, width, chans)
     values = tile.astype(F32)
@@ -97,9 +125,9 @@
 
     pl.semaphore_wait(barrier, n - 1)
 
-    send_stats(0)
+    visit_all(functools.partial(send_stats, 0))
     for d in range(1, nh):
-        there = {"seq": s, "ch": (h + d) % nh, "col": k}
+        there = {"seq": s, "ch": wrap(h + d, nh), "col": k}
         send(params.at[h], params.at[h], par_send, par_recv, there)
 
     def near(steps, ring):
@@ -112,10 +140,10 @@
         def ring(slot=slot):
             steps = 1 - slot
             for d in range(0 if steps else 1, nh):
-                there = {"seq": s + steps, "ch": (h + d) % nh, "col": k}
+                there = {"seq": s + steps, "ch": wrap(h + d, nh), "col": k}
                 send(lat.at[1, h], lat.at[slot, h], lat_send.at[slot], lat_recv.at[slot], there)
             for d in range(nh):
-                there = {"seq": s + steps, "ch": (h + d) % nh, "col": other}
+                there = {"seq": s + steps, "ch": wrap(h + d, nh), "col": other}
                 send(lat_edge_src, lat_edge.at[slot, h], late_send.at[slot], late_recv.at[slot], there)
         near(1 - slot, ring)
 
@@ -202,19 +230,16 @@
     own_stats(1, values)
     slot_here = h * ns + s
 
-    def send_mid(i):
-        q = (slot_here + i + 1) % pairs
-        send(mid_src.at[pl.ds(q % ns, 2)], mid.at[slot_here], mid_send, mid_recv,
-             {"seq": q % ns, "ch": q // ns, "col": k})
-
-    def send_mid_edge(i):
-        q = (slot_here + i) % pairs
-        send(mid_edge_src.at[pl.ds(q % ns, 2)], mid_edge.at[slot_here], mide_send, mide_recv,
-             {"seq": q % ns, "ch": q // ns, "col": other})
-
-    each(pairs - 1, send_mid)
-    each(pairs, send_mid_edge)
-    send_stats(1)
+    def send_mid(row, dh, dk):
+        send_stats(1, row, dh, dk)
+        if dk == 0:
+            others(row, dh, dk, lambda: send(
+                mid_src.at[pl.ds(row, 2)], mid.at[slot_here], mid_send, mid_recv, place_of(row, dh, dk)))
+        else:
+            send(mid_edge_src.at[pl.ds(row, 2)], mid_edge.at[slot_here], mide_send, mide_recv,
+                 place_of(row, dh, dk))
+
+    visit_all(send_mid)
     mid[slot_here] = mid_src[pl.ds(s, 2)]
 
     terms = norm_terms(1, frames * width * group_size * spread_over)
@@ -241,17 +266,17 @@
     hid_src[...] = tile
     hid_edge_src[...] = edge_of(values)
     own_stats(2, values)
+    visit_all(functools.partial(send_stats, 2))
     for slot in (1, 0):
         def ring(slot=slot):
             steps = 1 - slot
             for d in range(0 if steps else 1, nh):
-                there = {"seq": s + steps, "ch": (h + d) % nh, "col": k}
+                there = {"seq": s + steps, "ch": wrap(h + d, nh), "col": k}
                 send(hid_src, hid.at[slot, h], hid_send.at[slot], hid_recv.at[slot], there)
             for d in range(nh):
-                there = {"seq": s + steps, "ch": (h + d) % nh, "col": other}
+                there = {"seq": s + steps, "ch": wrap(h + d, nh), "col": other}
                 send(hid_edge_src, hid_edge.at[slot, h], hide_send.at[slot], hide_recv.at[slot], there)
         near(1 - slot, ring)
-    send_stats(2)
     hid[1, h] = tile
 
     terms = norm_terms(2, 2 * rows * width * group_size * spread_over)
@@ -323,10 +348,11 @@
         taps = mid_weight.shape
         return pl.pallas_call(
             functools.partial(kernel, sizes),
-            out_shape=jax.ShapeDtypeStruct((2, rows, width, chans), BF16),
-            in_specs=[vmem] * 10 + [hbm] * 3,
+            out_shape=pltpu.VMEM((2, rows, width, chans), BF16),
+            in_specs=[hbm] * 13,
             out_specs=vmem,
             scratch_shapes=[
+                pltpu.VMEM(latent.shape, BF16), *[pltpu.VMEM((chans,), F32)] * 9, dma((10,)),
                 pltpu.VMEM(taps, BF16), pltpu.VMEM(taps, BF16), pltpu.VMEM(taps, BF16), dma((3, 3)),
                 pltpu.VMEM((3, frames + 2, 3, width, full), F32),
                 pltpu.VMEM((3, 2, rows + 2, width, full), F32),

time: 29 us -> 30.2 us (1.041)
  Pallas kernels: 27.4 us -> 29.3 us
  local copies, waits for them, and re-layouts: 1.38 us -> 0.62 us
    pallas_call x1, Pallas kernels: 27.4 us -> 29.3 us  [body(): pl.pallas_call(functools.partial(kernel, sizes), out_shape=pltpu.VMEM((2,...]
    unnamed x1, local copies, waits for them, and re-layouts: 1.38 us -> 0.62 us
where the time goes in v2:
time: 30.2 us; the launch traced here: 30 us
  Pallas kernels  29.3 us (97%)
  local copies, waits for them, and re-layouts  0.62 us (2%)
    pallas_call x1, Pallas kernels, body(): pl.pallas_call(functools.partial(kernel, sizes), out_shape=pltpu.VMEM((2,...  29.3 us
    unnamed x1, local copies, waits for them, and re-layouts  0.62 us

profile of v2, /device:TPU:0, one launch (start us, length us, event | category | flops | bytes accessed | tf_op | source)
XLA Modules:
  0.0 30.0 jit_solution(9187545141663005299)
XLA Ops:
  0.0 29.3 %shard_map.127 = bf16[2,4,8,256]{3,2,1,0:T(8,128)(2,1)S(1)} custom-call(bf16[4,1,8,256]{3,2,1,0:T(8,128)(2,1)} %refs_0_.1, f32[256]{0:T(256)} %refs_1_.1, f32[256]{0:T(256)} %refs_2_.1, f32[256]{0:T(256)} %refs_3_.1, f32[256]{0:T(256)} %refs_4_.1, f32[256]{0:T(256)} %refs_5_.1, f32[256]{0:T(256)} %refs_6_.1, f32[256]{0:T(256)} %refs_7_.1, f32[256]{0:T(256)} %refs_8_.1, ...), custom_call_target="tpu_custom_call" | custom-call | tf_op jit(solution)/shard_map/pallas_call | solution.py:349
  29.3 0.6 %copy.15 = bf16[2,4,8,256]{3,2,1,0:T(8,128)(2,1)} copy(bf16[2,4,8,256]{3,2,1,0:T(8,128)(2,1)S(1)} %shard_map.127) | data formatting | bytes 65536

commit v3 on v2

--- a/solution.py
+++ b/solution.py
@@ -83,13 +83,6 @@
         load.start()
         small_loads.append(load)
 
-    loads = []
-    for c, (source, target) in enumerate(((mid_weight, w0), (first_weight, w1), (second_weight, w2))):
-        for dt in range(3):
-            load = pltpu.make_async_copy(source.at[dt], target.at[dt], w_sem.at[c, dt])
-            load.start()
-            loads.append(load)
-
     def send(src, dst, send_sem, recv_sem, where):
         pltpu.make_async_remote_copy(
             src_ref=src, dst_ref=dst, send_sem=send_sem, recv_sem=recv_sem,
@@ -146,6 +139,13 @@
                 there = {"seq": s + steps, "ch": wrap(h + d, nh), "col": other}
                 send(lat_edge_src, lat_edge.at[slot, h], late_send.at[slot], late_recv.at[slot], there)
         near(1 - slot, ring)
+
+    loads = []
+    for c, (source, target) in enumerate(((mid_weight, w0), (first_weight, w1), (second_weight, w2))):
+        for dt in range(3):
+            load = pltpu.make_async_copy(source.at[dt], target.at[dt], w_sem.at[c, dt])
+            load.start()
+            loads.append(load)
 
     act0[...] = jnp.zeros_like(act0)
     act1[...] = jnp.zeros_like(act1)

time: 30.2 us -> 26 us (0.86)
  Pallas kernels: 29.3 us -> 25.1 us
    pallas_call x1, Pallas kernels: 29.3 us -> 25.1 us  [body(): pl.pallas_call(functools.partial(kernel, sizes), out_shape=pltpu.VMEM((2,...]
where the time goes in v3:
time: 26 us; the launch traced here: 25.8 us
  Pallas kernels  25.1 us (97%)
  local copies, waits for them, and re-layouts  0.62 us (2%)
    pallas_call x1, Pallas kernels, body(): pl.pallas_call(functools.partial(kernel, sizes), out_shape=pltpu.VMEM((2,...  25.1 us
    unnamed x1, local copies, waits for them, and re-layouts  0.62 us

profile of v3, /device:TPU:0, one launch (start us, length us, event | category | flops | bytes accessed | tf_op | source)
XLA Modules:
  0.0 25.8 jit_solution(3744747976747762882)
XLA Ops:
  0.0 25.1 %shard_map.127 = bf16[2,4,8,256]{3,2,1,0:T(8,128)(2,1)S(1)} custom-call(bf16[4,1,8,256]{3,2,1,0:T(8,128)(2,1)} %refs_0_.1, f32[256]{0:T(256)} %refs_1_.1, f32[256]{0:T(256)} %refs_2_.1, f32[256]{0:T(256)} %refs_3_.1, f32[256]{0:T(256)} %refs_4_.1, f32[256]{0:T(256)} %refs_5_.1, f32[256]{0:T(256)} %refs_6_.1, f32[256]{0:T(256)} %refs_7_.1, f32[256]{0:T(256)} %refs_8_.1, ...), custom_call_target="tpu_custom_call" | custom-call | tf_op jit(solution)/shard_map/pallas_call | solution.py:349
  25.1 0.6 %copy.15 = bf16[2,4,8,256]{3,2,1,0:T(8,128)(2,1)} copy(bf16[2,4,8,256]{3,2,1,0:T(8,128)(2,1)S(1)} %shard_map.127) | data formatting | bytes 65536
